TPU v7x, 32 devices: a whole 2x2x4 slice. The times are simulated.
32 devices in a mesh: expert: 4 (over y, core), tensor: 8 (over z, x).
Axes of the slice: x: 2, y: 2, z: 4, core: 2. Of those that a mesh axis runs over, the one named last changes fastest.
Arguments:
- tokens: bfloat16 [1024, 6144], P('expert'), may hold values from -6 to 6
- expert_ids: int32 [1024, 2], P('expert'), may hold values from 0 to 3, all different within a row; in each aligned block of 256 rows (0 to 255, 256 to 511, ...) at most 192 rows name the same one
- gate_weights: float32 [1024, 2], P('expert'), may hold values from 0.2 to 1
- w_gate: bfloat16 [4, 6144, 16384], P('expert', None, 'tensor'), may hold values from -0.078125 to 0.078125
- w_up: bfloat16 [4, 6144, 16384], P('expert', None, 'tensor'), may hold values from -0.078125 to 0.078125
- w_down: bfloat16 [4, 16384, 6144], P('expert', 'tensor'), may hold values from -0.0625 to 0.0625
Outputs:
- mixed: bfloat16 [1024, 6144], P(('expert', 'tensor'))
Inputs may be any that keep to these rules, and one draw needn't show every extreme that they name: `expert_ids`: each token names two different experts. Among the 256 tokens held at one index along `expert`, no expert is named by more than 192 tokens, and in some such blocks one expert is named by exactly 192.
All inputs are finite; a program needn't handle non-finite values.
Results may differ from a plain program's by a relative error of at most 0.005.
Values may be sent and summed in bfloat16 or wider, within the bound.
A program may use at most 192 MiB of HBM per device.

v0:
```python
import jax
import jax.numpy as jnp
from jax import lax
from jax.sharding import PartitionSpec as P


def body(tokens, expert_ids, gate_weights, w_gate, w_up, w_down):
    tok_rows = tokens.shape[0]
    width = tokens.shape[1]
    groups = lax.axis_size("expert")
    capacity = 3 * tok_rows // 4
    slot_count = groups * capacity
    pair_hot = (
        expert_ids[:, :, None] == jnp.arange(groups, dtype=jnp.int32)[None, None, :]
    ).astype(jnp.int32)
    flat_hot = pair_hot.reshape(2 * tok_rows, groups)
    earlier = jnp.cumsum(flat_hot, axis=0) - flat_hot
    slot_rank = jnp.sum(earlier * flat_hot, axis=1)
    slot_index = expert_ids.reshape(-1) * capacity + slot_rank
    matched = (slot_index[None, :] == jnp.arange(slot_count, dtype=jnp.int32)[:, None]).astype(
        jnp.int32
    )
    matched = matched.reshape(slot_count, tok_rows, 2)
    taken = jnp.sum(matched, axis=2)
    slot_token = jnp.sum(taken * jnp.arange(tok_rows, dtype=jnp.int32)[None, :], axis=1)
    filled = jnp.sum(taken, axis=1) > 0
    combine = jnp.sum(matched.astype(jnp.float32) * gate_weights[None, :, :], axis=2)
    outgoing = jnp.where(filled[:, None], tokens[slot_token], jnp.zeros((), jnp.bfloat16))
    outgoing = outgoing.reshape(groups, capacity, width)
    arrived = lax.all_to_all(outgoing, "expert", split_axis=0, concat_axis=0, tiled=True)
    inputs = arrived.reshape(slot_count, width)
    gate_proj = jnp.dot(inputs, w_gate[0], preferred_element_type=jnp.float32)
    up_proj = jnp.dot(inputs, w_up[0], preferred_element_type=jnp.float32)
    hidden = (jax.nn.silu(gate_proj) * up_proj).astype(jnp.bfloat16)
    down_local = w_down[0]
    partial_value = lax.dot_general(
        down_local, hidden, (((0,), (1,)), ((), ())), preferred_element_type=jnp.float32
    )
    returned = lax.all_to_all(partial_value, "expert", split_axis=1, concat_axis=1, tiled=True)
    mixed_part = jnp.dot(returned, combine, precision=lax.Precision.HIGHEST)
    summed = lax.psum_scatter(mixed_part, "tensor", scatter_dimension=1, tiled=True)
    return summed.T.astype(jnp.bfloat16)


def solution(mesh):
    placed = (
        P("expert", None),
        P("expert", None),
        P("expert", None),
        P("expert", None, "tensor"),
        P("expert", None, "tensor"),
        P("expert", "tensor", None),
    )
    return jax.shard_map(
        body, mesh=mesh, in_specs=placed, out_specs=P(("expert", "tensor"), None), check_vma=False
    )
```

profile of v0, /device:TPU:0, one launch (start us, length us, event | category | flops | bytes accessed | tf_op | source)
XLA Modules:
  0.0 570.6 jit_solution(1858369969009648385)
XLA Ops:
  6.5 1.0 copy.19
  7.5 0.1 eq.44
  7.6 0.1 eq.40
  7.8 1.2 reduce-window.6
  9.0 0.2 slice_reduce_fusion
  9.2 0.2 reduce-window.9
  9.5 0.1 reduce_sum.50
  9.8 0.7 multiply_add_fusion
  10.5 0.2 convert_reduce_fusion.1
  10.7 0.2 multiply_reduce_fusion
  10.9 0.1 copy-done.2
  11.2 8.0 %gather_fusion = bf16[768,6144]{1,0:T(8,128)(2,1)} fusion(bf16[256,6144]{1,0:T(8,128)(2,1)S(1)} %copy-done, s32[1024]{0:T(1024)S(1)} %pad_clamp_fusion), kind=kCustom, calls=%fused_computation | custom fusion | bytes 18877440 | tf_op jit(solution)/shard_map/gather | solution.py:28
  19.2 8.1 %broadcast_select_fusion = bf16[4,192,6144]{2,1,0:T(8,128)(2,1)} fusion(bf16[4,192,6144]{2,1,0:T(8,128)(2,1)} %bitcast.43, pred[4,192]{1,0:T(4,128)(4,1)S(1)} %gt.11), kind=kLoop, calls=%fused_computation.7 | loop fusion | flops 4718592 | bytes 18875136 | tf_op jit(solution)/shard_map/jit(_where)/select_n | solution.py:28
  27.3 109.4 %all_to_all.17 = bf16[4,192,6144]{2,1,0:T(8,128)(2,1)S(1)} all-to-all(bf16[4,192,6144]{2,1,0:T(8,128)(2,1)} %broadcast_select_fusion), channel_id=1, replica_groups=mesh['expert'=4,'tensor'=8] {'expert'}, dimensions={0} | all-to-all | bytes 18874368 | tf_op jit(solution)/shard_map/all_to_all | solution.py:30
  136.6 23.2 %fusion.4 = f32[768,2048]{1,0:T(8,128)S(1)} fusion(bf16[768,6144]{1,0:T(8,128)(2,1)S(1)} %bitcast.45, bf16[1,6144,2048]{2,1,0:T(8,128)(2,1)} %param.9), kind=kOutput, calls=%fused_computation.5 | convolution fusion | flops 19327352832 | bytes 40894464 | tf_op jit(solution)/shard_map/dot_general | solution.py:32
  159.8 23.7 %multiply_convert_fusion = bf16[768,2048]{1,0:T(8,128)(2,1)S(1)} fusion(f32[768,2048]{1,0:T(8,128)S(1)} %fusion.4, bf16[768,6144]{1,0:T(8,128)(2,1)S(1)} %bitcast.46, bf16[1,6144,2048]{2,1,0:T(8,128)(2,1)} %param.10), kind=kOutput, calls=%fused_computation.8 | convolution fusion | flops 19336790016 | bytes 44040192 | tf_op jit(solution)/shard_map/dot_general | solution.py:33
  183.6 25.1 %fusion = f32[768,6144]{1,0:T(8,128)} fusion(bf16[768,2048]{1,0:T(8,128)(2,1)S(1)} %multiply_convert_fusion, bf16[1,2048,6144]{2,1,0:T(8,128)(2,1)} %param.11), kind=kOutput, calls=%fused_computation.1 | convolution fusion | flops 19327352832 | bytes 47185920 | tf_op jit(solution)/shard_map/dot_general | solution.py:36
  208.7 7.5 %all-to-all-start.1 = ((f32[6144,4,192]{0,2,1:T(8,128)}), f32[6144,4,192]{0,2,1:T(8,128)}, u32[]{:S(2)}, u32[]{:S(2)}) async-start(f32[6144,4,192]{0,2,1:T(8,128)} %bitcast.44), calls=%async_computation.1 | async-start | bytes 37748736 | tf_op jit(solution)/shard_map/all_to_all | solution.py:39
  216.2 0.3 reduce-scatter.2.cloned.1.call-start
  216.5 1.2 fusion.9
  217.7 204.0 %all-to-all-done.1 = f32[6144,4,192]{0,2,1:T(8,128)} async-done(((f32[6144,4,192]{0,2,1:T(8,128)}), f32[6144,4,192]{0,2,1:T(8,128)}, u32[]{:S(2)}, u32[]{:S(2)}) %all-to-all-start.1) | async-done | bytes 18874400 | tf_op jit(solution)/shard_map/all_to_all | solution.py:39
  421.7 21.1 %fusion.15 = f32[6144,256]{0,1:T(8,128)} fusion(f32[6144,768]{0,1:T(8,128)} %bitcast.8, f32[768,256]{1,0:T(8,128)} %fusion.9), kind=kOutput, calls=%fused_computation.31 | convolution fusion | flops 14495514624 | bytes 25952256 | tf_op jit(solution)/shard_map/dot_general | solution.py:40
  442.8 119.1 %reduce-scatter.2.cloned.1.call-done = f32[6144,32]{0,1:T(8,128)} async-done(((f32[6144,256]{0,1:T(8,128)}), f32[6144,32]{0,1:T(8,128)}) %reduce-scatter.2.cloned.1.call-update) | async-done | bytes 786448 | tf_op jit(solution)/shard_map/reduce_scatter | solution.py:41
  561.9 1.9 convert_bitcast_fusion
  (18 shorter events, 0.3 us)
Async XLA Ops:
  6.5 4.6 copy-start
  10.5 0.6 copy-start.2
  208.7 7.8 %copy-start.3 = (s32[256,2]{0,1:T(2,128)S(1)}, s32[256,2]{0,1:T(2,128)}, u32[]{:S(2)}) copy-start(s32[256,2]{0,1:T(2,128)} %copy-done.2) | copy-start | bytes 6148
  208.7 7.8 %copy-start.4 = (f32[256,2]{0,1:T(2,128)S(1)}, f32[256,2]{0,1:T(2,128)}, u32[]{:S(2)}) copy-start(f32[256,2]{0,1:T(2,128)} %param.8) | copy-start | bytes 6148
  208.7 213.0 %all-to-all-start.1 = ((f32[6144,4,192]{0,2,1:T(8,128)}), f32[6144,4,192]{0,2,1:T(8,128)}, u32[]{:S(2)}, u32[]{:S(2)}) async-start(f32[6144,4,192]{0,2,1:T(8,128)} %bitcast.44), calls=%async_computation.1 | async-start | bytes 37748736 | tf_op jit(solution)/shard_map/all_to_all | solution.py:39
  216.2 345.7 %reduce-scatter.2.cloned.1.call-start = ((), (), s32[]{:S(2)}) async-start(), calls=%async_computation.3 | async-start | bytes 7077888 | tf_op jit(solution)/shard_map/reduce_scatter | solution.py:41
  421.7 142.1 %copy-start.1 = (bf16[256,6144]{1,0:T(8,128)(2,1)S(1)}, bf16[256,6144]{1,0:T(8,128)(2,1)}, u32[]{:S(2)}) copy-start(bf16[256,6144]{1,0:T(8,128)(2,1)} %param.6) | copy-start | bytes 9437188
Sparse Core Ops, SparseCore 0:
  442.9 118.9 reduce-scatter.1
where the time goes:
time: 571 us
  waiting for transfers between devices  323 us (57%)
  blocking collectives  109 us (19%)
  matrix products  93.1 us (16%)
  other arithmetic  13.9 us (2%)
  between operations  13.5 us (2%)
  local copies, waits for them, and re-layouts  9.94 us (2%)
  starting transfers between devices  7.73 us (1%)
    all_to_all x1, waiting for transfers between devices, body(): lax.all_to_all(partial_value, 'expert', split_axis=1, concat_axis=1, tile...  204 us
    reduce_scatter x1, waiting for transfers between devices, body(): lax.psum_scatter(mixed_part, 'tensor', scatter_dimension=1, tiled=True)  119 us
    all_to_all x1, blocking collectives, body(): lax.all_to_all(outgoing, 'expert', split_axis=0, concat_axis=0, tiled=True)  109 us
    dot_general x1, matrix products, body(): lax.dot_general(down_local, hidden, (((0,), (1,)), ((), ())), preferred_e...  25.1 us
    dot_general x1, matrix products, body(): up_proj = jnp.dot(inputs, w_up[0], preferred_element_type=jnp.float32)  23.7 us
    dot_general x1, matrix products, body(): gate_proj = jnp.dot(inputs, w_gate[0], preferred_element_type=jnp.float32)  23.2 us
    dot_general x1, matrix products, body(): mixed_part = jnp.dot(returned, combine, precision=lax.Precision.HIGHEST)  21.1 us
  transfers between devices with their start and end apart: 2, of which 2 were waited for; matrix products, arithmetic and copies ran while one was open for 0% of the time, Pallas kernels for 0%

commit v1 on v0

--- a/solution.py
+++ b/solution.py
@@ -36,7 +36,10 @@
     partial_value = lax.dot_general(
         down_local, hidden, (((0,), (1,)), ((), ())), preferred_element_type=jnp.float32
     )
-    returned = lax.all_to_all(partial_value, "expert", split_axis=1, concat_axis=1, tiled=True)
+    size = lax.axis_size("expert")
+    blocks = jnp.stack(jnp.split(partial_value, size, axis=1), axis=0)
+    blocks = lax.all_to_all(blocks, "expert", split_axis=0, concat_axis=0)
+    returned = jnp.concatenate(blocks, axis=1)
     mixed_part = jnp.dot(returned, combine, precision=lax.Precision.HIGHEST)
     summed = lax.psum_scatter(mixed_part, "tensor", scatter_dimension=1, tiled=True)
     return summed.T.astype(jnp.bfloat16)

time: 571 us -> 589 us (1.032)
  local copies, waits for them, and re-layouts: 9.94 us -> 19.4 us
  other arithmetic: 13.9 us -> 22.5 us
    another operation x0 -> x1, local copies, waits for them, and re-layouts: none -> 9.48 us  [body(): blocks = jnp.stack(jnp.split(partial_value, size, axis=1), axis=0)]
    another operation x2 -> x3, other arithmetic: 1.41 us -> 10 us  [the longest x1 8.62 us: body(): blocks = jnp.stack(jnp.split(partial_value, size, axis=1), axis=0)]
where the time goes in v1:
time: 589 us
  waiting for transfers between devices  323 us (55%)
  blocking collectives  109 us (19%)
  matrix products  93.1 us (16%)
  other arithmetic  22.5 us (4%)
  local copies, waits for them, and re-layouts  19.4 us (3%)
  between operations  13.5 us (2%)
  starting transfers between devices  7.73 us (1%)
    all_to_all x1, waiting for transfers between devices, body(): blocks = lax.all_to_all(blocks, 'expert', split_axis=0, concat_axis=0)  204 us
    reduce_scatter x1, waiting for transfers between devices, body(): lax.psum_scatter(mixed_part, 'tensor', scatter_dimension=1, tiled=True)  119 us
    all_to_all x1, blocking collectives, body(): lax.all_to_all(outgoing, 'expert', split_axis=0, concat_axis=0, tiled=True)  109 us
    dot_general x1, matrix products, body(): lax.dot_general(down_local, hidden, (((0,), (1,)), ((), ())), preferred_e...  25.1 us
    dot_general x1, matrix products, body(): up_proj = jnp.dot(inputs, w_up[0], preferred_element_type=jnp.float32)  23.7 us
    dot_general x1, matrix products, body(): gate_proj = jnp.dot(inputs, w_gate[0], preferred_element_type=jnp.float32)  23.2 us
    dot_general x1, matrix products, body(): mixed_part = jnp.dot(returned, combine, precision=lax.Precision.HIGHEST)  21.1 us
  transfers between devices with their start and end apart: 2, of which 2 were waited for; matrix products, arithmetic and copies ran while one was open for 0% of the time, Pallas kernels for 0%

profile of v1, /device:TPU:0, one launch (start us, length us, event | category | flops | bytes accessed | tf_op | source)
XLA Modules:
  0.0 588.7 jit_solution(2586653806536580594)
XLA Ops:
  6.5 1.0 copy.19
  7.5 0.1 eq.44
  7.8 1.2 reduce-window.6
  9.0 0.2 slice_reduce_fusion
  9.2 0.2 reduce-window.9
  9.8 0.7 multiply_add_fusion
  10.5 0.2 convert_reduce_fusion.1
  10.7 0.2 multiply_reduce_fusion
  10.9 0.1 copy-done.2
  11.2 8.0 %gather_fusion = bf16[768,6144]{1,0:T(8,128)(2,1)} fusion(bf16[256,6144]{1,0:T(8,128)(2,1)S(1)} %copy-done, s32[1024]{0:T(1024)S(1)} %pad_clamp_fusion), kind=kCustom, calls=%fused_computation | custom fusion | bytes 18877440 | tf_op jit(solution)/shard_map/gather | solution.py:28
  19.2 8.1 %broadcast_select_fusion = bf16[4,192,6144]{2,1,0:T(8,128)(2,1)} fusion(bf16[4,192,6144]{2,1,0:T(8,128)(2,1)} %bitcast.54, pred[4,192]{1,0:T(4,128)(4,1)S(1)} %gt.11), kind=kLoop, calls=%fused_computation.9 | loop fusion | flops 4718592 | bytes 18875136 | tf_op jit(solution)/shard_map/jit(_where)/select_n | solution.py:28
  27.3 109.4 %all_to_all.10 = bf16[4,192,6144]{2,1,0:T(8,128)(2,1)S(1)} all-to-all(bf16[4,192,6144]{2,1,0:T(8,128)(2,1)} %broadcast_select_fusion), channel_id=1, replica_groups=mesh['expert'=4,'tensor'=8] {'expert'}, dimensions={0} | all-to-all | bytes 18874368 | tf_op jit(solution)/shard_map/all_to_all | solution.py:30
  136.6 23.2 %fusion.4 = f32[768,2048]{1,0:T(8,128)S(1)} fusion(bf16[768,6144]{1,0:T(8,128)(2,1)S(1)} %bitcast.55, bf16[1,6144,2048]{2,1,0:T(8,128)(2,1)} %param.9), kind=kOutput, calls=%fused_computation.5 | convolution fusion | flops 19327352832 | bytes 40894464 | tf_op jit(solution)/shard_map/dot_general | solution.py:32
  159.8 23.7 %multiply_convert_fusion = bf16[768,2048]{1,0:T(8,128)(2,1)S(1)} fusion(f32[768,2048]{1,0:T(8,128)S(1)} %fusion.4, bf16[768,6144]{1,0:T(8,128)(2,1)S(1)} %bitcast.56, bf16[1,6144,2048]{2,1,0:T(8,128)(2,1)} %param.10), kind=kOutput, calls=%fused_computation.10 | convolution fusion | flops 19336790016 | bytes 44040192 | tf_op jit(solution)/shard_map/dot_general | solution.py:33
  183.6 25.1 %fusion.6 = f32[6144,768]{0,1:T(8,128)} fusion(bf16[768,2048]{1,0:T(8,128)(2,1)S(1)} %multiply_convert_fusion, bf16[1,2048,6144]{2,1,0:T(8,128)(2,1)} %param.11), kind=kOutput, calls=%fused_computation.8 | convolution fusion | flops 19327352832 | bytes 47185920 | tf_op jit(solution)/shard_map/dot_general | solution.py:36
  208.7 9.5 %slice_bitcast_fusion.3 = (f32[1,6144,192]{1,2,0:T(8,128)S(1)}, f32[1,6144,192]{1,2,0:T(8,128)S(1)}, f32[1,6144,192]{1,2,0:T(8,128)S(1)}, f32[1,6144,192]{1,2,0:T(8,128)}) fusion(f32[6144,768]{0,1:T(8,128)} %fusion.6), kind=kLoop, calls=%fused_computation.14 | loop fusion | bytes 37748736 | tf_op jit(solution)/shard_map/stack | solution.py:40
  218.2 8.6 %pad_maximum_fusion = f32[4,6144,192]{1,2,0:T(8,128)} fusion(f32[1,6144,192]{1,2,0:T(8,128)S(1)} %get-tuple-element.8, f32[1,6144,192]{1,2,0:T(8,128)S(1)} %get-tuple-element.9, f32[1,6144,192]{1,2,0:T(8,128)} %get-tuple-element.10, f32[1,6144,192]{1,2,0:T(8,128)S(1)} %get-tuple-element.7), kind=kLoop, calls=%fused_computation.7 | loop fusion | flops 14155776 | bytes 37748736 | tf_op jit(solution)/shard_map/stack | solution.py:40
  226.8 7.5 %all-to-all-start.1 = ((f32[4,6144,192]{1,2,0:T(8,128)}), f32[4,6144,192]{1,2,0:T(8,128)}, u32[]{:S(2)}, u32[]{:S(2)}) async-start(f32[4,6144,192]{1,2,0:T(8,128)} %pad_maximum_fusion), calls=%async_computation.1 | async-start | bytes 37748736 | tf_op jit(solution)/shard_map/all_to_all | solution.py:41
  234.3 0.3 reduce-scatter.2.cloned.1.call-start
  234.6 1.2 fusion.12
  235.8 204.0 %all-to-all-done.1 = f32[4,6144,192]{1,2,0:T(8,128)} async-done(((f32[4,6144,192]{1,2,0:T(8,128)}), f32[4,6144,192]{1,2,0:T(8,128)}, u32[]{:S(2)}, u32[]{:S(2)}) %all-to-all-start.1) | async-done | bytes 18874400 | tf_op jit(solution)/shard_map/all_to_all | solution.py:41
  439.8 21.1 %fusion.18 = f32[6144,256]{0,1:T(8,128)} fusion(f32[6144,768]{0,1:T(8,128)} %bitcast.12, f32[768,256]{1,0:T(8,128)} %fusion.12), kind=kOutput, calls=%fused_computation.37 | convolution fusion | flops 14495514624 | bytes 25952256 | tf_op jit(solution)/shard_map/dot_general | solution.py:43
  460.9 119.1 %reduce-scatter.2.cloned.1.call-done = f32[6144,32]{0,1:T(8,128)} async-done(((f32[6144,256]{0,1:T(8,128)}), f32[6144,32]{0,1:T(8,128)}) %reduce-scatter.2.cloned.1.call-update) | async-done | bytes 786448 | tf_op jit(solution)/shard_map/reduce_scatter | solution.py:44
  580.0 1.9 convert_bitcast_fusion
  (20 shorter events, 0.6 us)
Async XLA Ops:
  6.5 4.6 copy-start
  10.5 0.6 copy-start.2
  226.8 7.8 %copy-start.3 = (s32[256,2]{0,1:T(2,128)S(1)}, s32[256,2]{0,1:T(2,128)}, u32[]{:S(2)}) copy-start(s32[256,2]{0,1:T(2,128)} %copy-done.2) | copy-start | bytes 6148
  226.8 7.8 %copy-start.4 = (f32[256,2]{0,1:T(2,128)S(1)}, f32[256,2]{0,1:T(2,128)}, u32[]{:S(2)}) copy-start(f32[256,2]{0,1:T(2,128)} %param.8) | copy-start | bytes 6148
  226.8 213.0 %all-to-all-start.1 = ((f32[4,6144,192]{1,2,0:T(8,128)}), f32[4,6144,192]{1,2,0:T(8,128)}, u32[]{:S(2)}, u32[]{:S(2)}) async-start(f32[4,6144,192]{1,2,0:T(8,128)} %pad_maximum_fusion), calls=%async_computation.1 | async-start | bytes 37748736 | tf_op jit(solution)/shard_map/all_to_all | solution.py:41
  234.3 345.7 %reduce-scatter.2.cloned.1.call-start = ((), (), s32[]{:S(2)}) async-start(), calls=%async_computation.3 | async-start | bytes 7077888 | tf_op jit(solution)/shard_map/reduce_scatter | solution.py:44
  439.8 142.1 %copy-start.1 = (bf16[256,6144]{1,0:T(8,128)(2,1)S(1)}, bf16[256,6144]{1,0:T(8,128)(2,1)}, u32[]{:S(2)}) copy-start(bf16[256,6144]{1,0:T(8,128)(2,1)} %param.6) | copy-start | bytes 9437188
Sparse Core Ops, SparseCore 0:
  461.0 118.9 reduce-scatter.1
